TPU v7x, 32 devices: a whole 2x2x4 slice. The times are simulated.
32 devices in a mesh: seq: 8 (over z, x), dp: 4 (over y, core).
Axes of the slice: x: 2, y: 2, z: 4, core: 2. Of those that a mesh axis runs over, the one named last changes fastest.
Arguments:
- conv_input: bfloat16 [4, 2048, 2816], P('dp', 'seq'), may hold values from -6 to 6
- gate_input: bfloat16 [4, 2048, 2560], P('dp', 'seq'), may hold values from -6 to 6
- step_input: float32 [4, 40, 2048], P('dp', None, 'seq'), may hold values from -7.5 to 2048
- filter_taps: float32 [4, 2816], replicated, may hold values from -3 to 3
- filter_bias: float32 [2816], replicated, may hold values from -0.5 to 0.5
- step_bias: float32 [40], replicated, may hold values from -1 to 1
- decay_log: float32 [40], replicated, may hold values from -13 to 3
- skip_gain: float32 [40], replicated, may hold values from 0.5 to 1.5
- norm_weight: float32 [2560], replicated, may hold values from 0.5 to 1.5
- output_weight: bfloat16 [2560, 1280], P('dp'), may hold values from -0.125 to 0.125
- output_grad: bfloat16 [4, 2048, 1280], P('dp', 'seq'), may hold values from -6 to 6
Outputs:
- input_grad: bfloat16 [4, 2048, 2816], P('dp', 'seq')
- gate_grad: bfloat16 [4, 2048, 2560], P('dp', 'seq')
- step_grad: float32 [4, 40, 2048], P('dp', None, 'seq')
- weight_grad: float32 [2560, 1280], P('dp')
- filter_grads: float32 [5, 2816], replicated
- norm_grad: float32 [2560], replicated
- head_grads: float32 [3, 40], replicated
All inputs are finite; a program needn't handle non-finite values.
Results may differ from a plain program's by a relative error of at most 0.0029.
Values may be sent and summed in bfloat16 or wider, within the bound.
No kernel may reach another device: no remote copies, remote signals or barrier semaphores. Data moves between devices by JAX's collectives and lax.ppermute only.
A program may use at most 192 MiB of HBM per device.

v0:
```python
import jax
import jax.numpy as jnp
from jax import lax
from jax.sharding import PartitionSpec as P

HEADS = 40
HEAD_DIM = 64
STATE = 128
SPAN = 256
INNER = 2560
HIGHEST = lax.Precision.HIGHEST
MASKED = -1e30
EPSILON = 1e-05


def passed_along(value, axis, steps):
    count = lax.axis_size(axis)
    first, last = (max(0, -steps), min(count, count - steps))
    return lax.ppermute(value, axis, [(source, source + steps) for source in range(first, last)])


def entering_2(value, axis, combine, identity, reverse):
    length, position = (lax.axis_size(axis), lax.axis_index(axis))
    everything = jax.tree.map(lambda part: lax.all_gather(part, axis), value)
    start = jax.tree.map(
        lambda part, zero: jnp.broadcast_to(jnp.asarray(zero, part.dtype), part.shape),
        value,
        identity,
    )

    def lap(k, before):
        at = length - 1 - k if reverse else k
        reached = at > position if reverse else at < position
        new = combine(before, jax.tree.map(lambda part: part[at], everything))
        return jax.tree.map(lambda a, b: jnp.where(reached, a, b), new, before)

    return lax.fori_loop(0, length, lap, start)


def affine(earlier, later):
    return (earlier[0] * later[0], later[0][:, None, None] * earlier[1] + later[1])


def prepare(extended, step_rows, filter_taps, filter_bias, step_bias, decay_log):
    width = filter_taps.shape[0]
    length = extended.shape[0] - width + 1
    filtered = filter_bias + filter_taps[0] * extended[0:length]
    for offset in range(1, width):
        filtered = filtered + filter_taps[offset] * extended[offset : offset + length]
    activated = jax.nn.silu(filtered)
    step_sizes = jax.nn.softplus(step_rows + step_bias[:, None])
    decay_rates = step_sizes * (-jnp.exp(decay_log))[:, None]
    blocks = length // SPAN
    cumsums = jnp.cumsum(decay_rates.reshape(HEADS, blocks, SPAN), axis=2)
    values = activated[:, :INNER].reshape(blocks, SPAN, HEADS, HEAD_DIM)
    key_side = activated[:, INNER : INNER + STATE].reshape(blocks, SPAN, STATE)
    scaled = values * step_sizes.reshape(HEADS, blocks, SPAN).transpose(1, 2, 0)[..., None]
    to_end = jnp.exp(cumsums[:, :, -1:] - cumsums)
    block_states = jnp.einsum("hcs,cshp,csn->chpn", to_end, scaled, key_side, precision=HIGHEST)
    decays = jnp.exp(cumsums[:, :, -1]).T
    return (activated, cumsums, scaled, block_states, decays)


def summarize(block_states, decays):
    product = jnp.ones((decays.shape[1],), jnp.float32)
    running = jnp.zeros(block_states.shape[1:], jnp.float32)
    running = decays[0][:, None, None] * running + block_states[0]
    product = product * decays[0]
    return (product, running)


def finish(
    activated, cumsums, scaled, block_states, decays, entering, skip_gain, gate_rows, norm_weight
):
    blocks = cumsums.shape[1]
    length = blocks * SPAN
    values = activated[:, :INNER].reshape(blocks, SPAN, HEADS, HEAD_DIM)
    key_side = activated[:, INNER : INNER + STATE].reshape(blocks, SPAN, STATE)
    query_side = activated[:, INNER + STATE :].reshape(blocks, SPAN, STATE)
    starting = []
    starting.append(entering)
    starting = jnp.stack(starting)
    scores = jnp.einsum("ctn,csn->cts", query_side, key_side, precision=HIGHEST)
    differences = cumsums[:, :, :, None] - cumsums[:, :, None, :]
    causal = jnp.tril(jnp.ones((SPAN, SPAN), dtype=bool))
    weights = scores[None] * jnp.exp(jnp.where(causal, differences, MASKED))
    inside = jnp.einsum("hcts,cshp->cthp", weights, scaled, precision=HIGHEST)
    from_state = (
        jnp.einsum("ctn,chpn->cthp", query_side, starting, precision=HIGHEST)
        * jnp.exp(cumsums).transpose(1, 2, 0)[..., None]
    )
    result = inside + from_state + skip_gain[:, None] * values
    scanned = result.reshape(length, INNER)
    gated = scanned * jax.nn.silu(gate_rows)
    inverse_rms = lax.rsqrt(jnp.mean(gated * gated, axis=1, keepdims=True) + EPSILON)
    return gated * inverse_rms * norm_weight


def body(
    conv_input,
    gate_input,
    step_input,
    filter_taps,
    filter_bias,
    step_bias,
    decay_log,
    skip_gain,
    norm_weight,
    output_weight,
    output_grad,
):
    kernel_rows = filter_taps.shape[0] - 1
    raw_rows = conv_input[0]
    before = passed_along(raw_rows[-kernel_rows:], "seq", 1)
    extended = jnp.concatenate([before, raw_rows], axis=0).astype(jnp.float32)
    gate_rows = gate_input[0].astype(jnp.float32)
    step_rows = step_input[0]
    cotangent = output_grad[0]
    tokens = cotangent.shape[0]
    primals, pull_first = jax.vjp(
        prepare, extended, step_rows, filter_taps, filter_bias, step_bias, decay_log
    )
    activated, cumsums, scaled, block_states, decays = primals
    summary, pull_summary = jax.vjp(summarize, block_states, decays)
    identity = (jnp.ones_like(summary[0]), jnp.zeros_like(summary[1]))
    _, entering = entering_2(summary, "seq", affine, identity, False)
    normed, pull_second = jax.vjp(
        finish,
        activated,
        cumsums,
        scaled,
        block_states,
        decays,
        entering,
        skip_gain,
        gate_rows,
        norm_weight,
    )
    normed_low = normed.astype(jnp.bfloat16)
    groups = lax.axis_size("dp")
    own_rows = output_weight.shape[0]
    partial_columns = lax.dot_general(
        lax.all_gather(cotangent, "dp", axis=0, tiled=True),
        output_weight,
        (((1,), (1,)), ((), ())),
        preferred_element_type=jnp.float32,
    )
    regrouped = partial_columns.reshape(groups, tokens, own_rows)
    normed_grad = lax.all_to_all(regrouped, "dp", split_axis=0, concat_axis=2, tiled=True).reshape(
        tokens, groups * own_rows
    )
    weight_piece = lax.psum_scatter(
        lax.dot_general(
            normed_low, cotangent, (((0,), (0,)), ((), ())), preferred_element_type=jnp.float32
        ),
        "dp",
        scatter_dimension=0,
        tiled=True,
    )
    weight_grad = lax.psum(weight_piece, "seq")
    second = pull_second(normed_grad)
    (
        grad_activated,
        grad_cumsums,
        grad_scaled,
        grad_states,
        grad_decays,
        grad_entering,
        grad_skip,
        grad_gate,
        grad_norm,
    ) = second
    _, end_grad = entering_2((summary[0], grad_entering), "seq", affine, identity, True)
    decay_grad = jnp.sum(end_grad * entering, axis=(1, 2))
    more_states, more_decays = pull_summary((decay_grad, end_grad))
    first = pull_first(
        (
            grad_activated,
            grad_cumsums,
            grad_scaled,
            grad_states + more_states,
            grad_decays + more_decays,
        )
    )
    grad_extended, grad_steps, grad_taps, grad_bias, grad_step_bias, grad_decay_log = first
    returned = passed_along(grad_extended[:kernel_rows], "seq", -1)
    own_part = grad_extended[kernel_rows:]
    own_part = jnp.concatenate(
        [own_part[:-kernel_rows], own_part[-kernel_rows:] + returned], axis=0
    )
    filter_part = jnp.concatenate([grad_taps, grad_bias[None]], axis=0)
    head_part = jnp.stack([grad_step_bias, grad_decay_log, grad_skip])
    filter_grads, norm_grad, head_grads = lax.psum(
        (filter_part, grad_norm, head_part), ("seq", "dp")
    )
    input_grad = own_part.astype(jnp.bfloat16)[None]
    gate_grad = grad_gate.astype(jnp.bfloat16)[None]
    step_grad = grad_steps[None]
    return (input_grad, gate_grad, step_grad, weight_grad, filter_grads, norm_grad, head_grads)


def solution(mesh):
    return jax.shard_map(
        body,
        mesh=mesh,
        in_specs=(
            P("dp", "seq", None),
            P("dp", "seq", None),
            P("dp", None, "seq"),
            P(),
            P(),
            P(),
            P(),
            P(),
            P(),
            P("dp", None),
            P("dp", "seq", None),
        ),
        out_specs=(
            P("dp", "seq", None),
            P("dp", "seq", None),
            P("dp", None, "seq"),
            P("dp", None),
            P(),
            P(),
            P(),
        ),
        check_vma=False,
    )
```

profile of v0, /device:TPU:0, one launch (start us, length us, event | category | flops | bytes accessed | tf_op | source)
XLA Modules:
  0.0 764.4 jit_solution(17478603161339498694)
XLA Ops:
  8.8 4.9 collective-permute-start
  20.2 3.0 fusion.21
  24.7 1.9 slice.95
  26.6 3.2 copy.94
  29.8 5.0 fusion.69
  34.8 3.0 all-gather.8.cloned.1.call-done
  37.9 5.5 fusion.48
  43.4 4.7 all-to-all-start
  49.6 22.7 %all-reduce.15 = f32[320]{0:T(512)S(1)} all-reduce(f32[320]{0:T(512)S(1)} %dynamic-update-slice), channel_id=3, replica_groups=mesh['seq'=8,'dp'=4] {'seq'}, use_global_device_ids=true, to_apply=%add.15 | all-reduce | flops 320 | bytes 2560
  72.4 1.8 copy.100
  75.7 3.6 all-to-all-done
  79.4 3.2 copy.93
  82.6 108.8 %all-gather.10.cloned.1.call-done = f32[320,64,128]{2,1,0:T(8,128)} async-done(((f32[40,64,128]{2,1,0:T(8,128)}), f32[320,64,128]{2,1,0:T(8,128)}) %all-gather.10.cloned.1.call-update) | async-done | bytes 10485776 | tf_op jit(solution)/shard_map/all_gather | solution.py:24
  191.4 13.2 %while.30 = (s32[]{:T(128)}, f32[40,64,128]{2,1,0:T(8,128)S(1)}, s32[]{:T(128)}, f32[8,40]{1,0:T(8,128)S(1)}, f32[8,40,64,128]{3,2,1,0:T(8,128)}, /*index=5*/s32[]{:T(128)}, s32[]{:T(128)}) while((s32[]{:T(128)}, f32[40,64,128]{2,1,0:T(8,128)S(1)}, s32[]{:T(128)}, f32[8,40]{1,0:T(8,128)S(1)}, f32[8,40,64,128]{3,2,1,0:T(8,128)}, ...), condition=%wide.region_3.4_spmd.clone, body=%wide.region_2.3_spmd.clone.sunk | while | flops 1310724 | bytes 3932745 | solution.py:37
  204.6 3.3 fusion.93
  208.0 15.5 %multiply_reduce_fusion.8 = (f32[256]{0:T(256)S(1)}, f32[256]{0:T(256)S(1)}, f32[1,256,40,64]{1,3,2,0:T(8,128)S(1)}, f32[1,256,40,64]{1,3,2,0:T(8,128)}) fusion(f32[1,256,40,64]{1,3,2,0:T(8,128)} %bitcast.259, f32[40,64]{1,0:T(8,128)S(1)} %mul.591, f32[1,256,40,64]{1,3,2,0:T(8,128)} %bitcast.262, f32[1,256,40,64]{1,3,2,0:T(8,128)S(1)} %bitcast.254, ...), kind=kOutput, calls=%fused_computation.79 | convolution fusion | flops 2030960128 | bytes 18813088 | tf_op jit(solution)/shard_map/jvp(hcts,cshp->cthp)/dot_general | solution.py:87
  223.5 2.6 broadcast_multiply_fusion.5
  227.6 4.2 fusion.44
  231.8 8.5 %fusion.86 = f32[2560,1280]{1,0:T(8,128)} fusion(bf16[256,2560]{0,1:T(8,128)(2,1)S(1)} %bitcast.268, bf16[1,256,1280]{2,1,0:T(8,128)(2,1)} %param.25), kind=kOutput, calls=%fused_computation.114 | convolution fusion | flops 1677721600 | bytes 15073280 | tf_op jit(solution)/shard_map/dot_general | solution.py:153
  240.7 3.2 convert_element_type.75
  243.9 3.7 copy.129
  247.6 15.7 %fusion.8 = (f32[40,256]{1,0:T(8,128)S(1)}, f32[40,256]{1,0:T(8,128)}, f32[256,256]{1,0:T(8,128)S(1)}) fusion(f32[40,256]{1,0:T(8,128)S(1)} %get-tuple-element.347, f32[256,256]{1,0:T(8,128)S(1)} %copy-done.19, pred[256,256]{1,0:T(8,128)(4,1)S(1)} %iota_compare_fusion, f32[256,40,64]{0,2,1:T(8,128)S(1)} %bitcast.256, f32[256,40]{0,1:T(8,128)S(1)} %fusion.106, ...), kind=kOutput, calls=%fused_computation.13 | convolution fusion | flops 2037428224 | bytes 5996544 | tf_op jit(solution)/shard_map/transpose(jvp(hcts,cshp->cthp))/dot_general | solution.py:87
  263.3 3.2 copy.101
  266.5 3.2 copy.117
  269.7 4.3 fusion.33
  274.7 3.3 copy.106
  279.6 6.0 fusion.83
  286.9 3.2 fusion.29
  290.1 90.5 %all-gather.12.cloned.1.call-done = f32[320,64,128]{2,1,0:T(8,128)} async-done(((f32[40,64,128]{2,1,0:T(8,128)}), f32[320,64,128]{2,1,0:T(8,128)}) %all-gather.12.cloned.1.call-update) | async-done | bytes 10485776 | tf_op jit(solution)/shard_map/all_gather | solution.py:24
  380.6 21.0 %while.31 = (s32[]{:T(128)}, f32[40,64,128]{2,1,0:T(8,128)S(1)}, s32[]{:T(128)}, f32[8,40]{1,0:T(8,128)}, f32[8,40,64,128]{3,2,1,0:T(8,128)}, /*index=5*/s32[]{:T(128)}, s32[]{:T(128)}, s32[]{:T(128)}, s32[]{:T(128)}) while((s32[]{:T(128)}, f32[40,64,128]{2,1,0:T(8,128)S(1)}, s32[]{:T(128)}, f32[8,40]{1,0:T(8,128)}, ...), condition=%wide.region_8.9_spmd.clone, body=%wide.region_7.8_spmd.clone.sunk | while | flops 1310728 | bytes 3932807 | solution.py:37
  386.0 2.0 fusion.138
  391.1 2.1 fusion.138
  393.9 2.1 fusion.138
  396.7 2.1 fusion.138
  399.5 1.7 fusion.138
  402.2 5.5 fusion.39
  408.7 2.5 reduce-window.16
  411.5 12.6 %multiply_reduce_fusion.5 = (f32[40]{0:T(128)S(1)}, f32[256,40]{0,1:T(8,128)S(1)}, f32[1,256,40,64]{1,3,2,0:T(8,128)}) fusion(f32[1,256,40,64]{1,3,2,0:T(8,128)} %copy-done.9, f32[1,256,40,64]{1,3,2,0:T(8,128)} %bitcast.252, f32[256,40]{0,1:T(8,128)S(1)} %fusion.106, f32[256,40]{0,1:T(8,128)S(1)} %get-tuple-element.346, ...), kind=kOutput, calls=%fused_computation.75 | convolution fusion | flops 2025707520 | bytes 10977440 | tf_op jit(solution)/shard_map/transpose(jvp(hcts,cshp->cthp))/dot_general | solution.py:87
  424.1 3.4 copy.103
  427.5 6.1 fusion.80
  433.7 6.0 multiply_reduce_fusion.4
  441.5 4.4 fusion.26
  445.9 38.5 %reduce-scatter.2.cloned.1.call-done = f32[640,1280]{1,0:T(8,128)} async-done(((f32[2560,1280]{1,0:T(8,128)}), f32[640,1280]{1,0:T(8,128)}) %reduce-scatter.2.cloned.1.call-update) | async-done | bytes 3276816 | tf_op jit(solution)/shard_map/reduce_scatter | solution.py:152
  484.4 2.7 broadcast_multiply_fusion.3
  490.8 2.4 collective-permute-done.1
  494.4 120.0 %all-reduce.22.cloned.1.call-done = (f32[5,2816]{1,0:T(8,128)}, f32[2560]{0:T(1024)}, f32[3,40]{1,0:T(4,128)}) async-done(((f32[5,2816]{1,0:T(8,128)}, f32[2560]{0:T(1024)}, f32[3,40]{1,0:T(4,128)}), (f32[5,2816]{1,0:T(8,128)}, f32[2560]{0:T(1024)}, f32[3,40]{1,0:T(4,128)})) %all-reduce.22.cloned.1.call-update) | async-done | bytes 67056 | tf_op jit(solution)/shard_map/psum | solution.py:193
  614.4 137.1 %all-reduce.20.cloned.1.call-done = f32[640,1280]{1,0:T(8,128)} async-done(((f32[640,1280]{1,0:T(8,128)}), f32[640,1280]{1,0:T(8,128)}) %all-reduce.20.cloned.1.call-update) | async-done | bytes 3276816 | tf_op jit(solution)/shard_map/psum | solution.py:160
  751.5 4.0 copy.175
  (174 shorter events, 51.1 us)
Async XLA Ops:
  7.2 30.7 %copy-start = (bf16[640,1280]{1,0:T(8,128)(2,1)S(1)}, bf16[640,1280]{1,0:T(8,128)(2,1)}, u32[]{:S(2)}) copy-start(bf16[640,1280]{1,0:T(8,128)(2,1)} %param.24) | copy-start | bytes 4915204
  7.2 12.7 %copy-start.16 = (bf16[1,256,2816]{2,1,0:T(8,128)(2,1)S(1)}, bf16[1,256,2816]{2,1,0:T(8,128)(2,1)}, u32[]{:S(2)}) copy-start(bf16[1,256,2816]{2,1,0:T(8,128)(2,1)} %param.15) | copy-start | bytes 4325380
  7.2 30.7 %all-gather.8.cloned.1.call-start = ((), (), s32[]{:S(2)}) async-start(), calls=%async_computation.4 | async-start | bytes 3276800 | tf_op jit(solution)/shard_map/all_gather | solution.py:143
  7.9 183.4 %all-gather.10.cloned.1.call-start = ((), (), s32[]{:S(2)}) async-start(), calls=%async_computation.5 | async-start | bytes 11796480 | tf_op jit(solution)/shard_map/all_gather | solution.py:24
  8.8 11.1 %collective-permute-start = (bf16[3,2816]{1,0:T(4,128)(2,1)S(1)}, bf16[3,2816]{1,0:T(4,128)(2,1)S(1)}, u32[]{:S(2)}, u32[]{:S(2)}) collective-permute-start(bf16[3,2816]{1,0:T(4,128)(2,1)S(1)} %slice_bitcast_fusion), channel_id=1, source_target_pairs={{0,4},{4,8},{8,12},{12,16},{16,20},{20,24},{24,28},{1,5},{5,9},{9,... | collective-permute-start | bytes 50696 | tf_op jit(solution)/shard_map/ppermute | solution.py:19
  16.5 3.7 copy-start.24
  20.2 3.0 copy-start.2
  23.2 1.6 copy-start.12
  43.4 4.8 copy-start.31
  43.4 29.1 %copy-start.13 = (bf16[1,256,2560]{2,1,0:T(8,128)(2,1)S(1)}, bf16[1,256,2560]{2,1,0:T(8,128)(2,1)}, u32[]{:S(2)}) copy-start(bf16[1,256,2560]{2,1,0:T(8,128)(2,1)} %param.16) | copy-start | bytes 3932164
  43.4 36.0 %all-to-all-start = ((f32[4,256,640]{2,1,0:T(8,128)}), f32[4,256,640]{2,1,0:T(8,128)}, u32[]{:S(2)}, u32[]{:S(2)}) async-start(f32[4,256,640]{2,1,0:T(8,128)} %bitcast.271), calls=%async_computation | async-start | bytes 5242880 | tf_op jit(solution)/shard_map/all_to_all | solution.py:149
  48.0 26.2 %copy-start.22 = (f32[2560]{0:T(1024)S(1)}, f32[2560]{0:T(1024)}, u32[]{:S(2)}) copy-start(f32[2560]{0:T(1024)} %param.23) | copy-start | bytes 30724
  48.0 332.6 %all-gather.12.cloned.1.call-start = ((), (), s32[]{:S(2)}) async-start(), calls=%async_computation.6 | async-start | bytes 11796480 | tf_op jit(solution)/shard_map/all_gather | solution.py:24
  75.7 132.2 %copy-start.18 = (f32[256,256]{1,0:T(8,128)}, f32[256,256]{1,0:T(8,128)S(1)}, u32[]{:S(2)}) copy-start(f32[256,256]{1,0:T(8,128)S(1)} %fusion.98) | copy-start | bytes 786436
  204.6 18.9 %copy-start.27 = (f32[8,40]{1,0:T(8,128)}, f32[8,40]{1,0:T(8,128)S(1)}, u32[]{:S(2)}) copy-start(f32[8,40]{1,0:T(8,128)S(1)} %get-tuple-element.516) | copy-start | bytes 3844
  204.6 3.3 copy-start.4
  204.6 3.3 copy-start.29
  207.9 15.6 %copy-start.15 = (f32[256,40,64]{0,2,1:T(8,128)}, f32[256,40,64]{0,2,1:T(8,128)S(1)}, u32[]{:S(2)}) copy-start(f32[256,40,64]{0,2,1:T(8,128)S(1)} %fusion.93) | copy-start | bytes 7864324
  207.9 15.6 %copy-start.7 = (f32[1,256,4,640]{1,3,2,0:T(8,128)S(1)}, f32[1,256,4,640]{1,3,2,0:T(8,128)}, u32[]{:S(2)}) copy-start(f32[1,256,4,640]{1,3,2,0:T(8,128)} %copy.93) | copy-start | bytes 7864324
  208.0 15.6 %copy-start.11 = (f32[1,256,2560]{1,2,0:T(8,128)S(1)}, f32[1,256,2560]{1,2,0:T(8,128)}, u32[]{:S(2)}) copy-start(f32[1,256,2560]{1,2,0:T(8,128)} %copy.100) | copy-start | bytes 7864324
  226.1 1.5 copy-start.9
  231.8 252.6 %reduce-scatter.2.cloned.1.call-start = ((), (), s32[]{:S(2)}) async-start(), calls=%async_computation.2 | async-start | bytes 16384000 | tf_op jit(solution)/shard_map/reduce_scatter | solution.py:152
  240.4 374.0 %all-reduce.22.cloned.1.call-start = ((), (), s32[]{:S(2)}) async-start(), calls=%async_computation.7 | async-start | bytes 208896 | tf_op jit(solution)/shard_map/psum | solution.py:193
  240.7 7.0 copy-start.19
  243.9 3.8 copy-start.5
  243.9 3.8 copy-start.10
  277.9 8.9 %copy-start.6 = (f32[1,256,40,64]{1,3,2,0:T(8,128)S(1)}, f32[1,256,40,64]{1,3,2,0:T(8,128)}, u32[]{:S(2)}) copy-start(f32[1,256,40,64]{1,3,2,0:T(8,128)} %get-tuple-element.358) | copy-start | bytes 7864324
  277.9 8.9 %copy-start.8 = (f32[1,256,4,640]{1,3,2,0:T(8,128)S(1)}, f32[1,256,4,640]{1,3,2,0:T(8,128)}, u32[]{:S(2)}) copy-start(f32[1,256,4,640]{1,3,2,0:T(8,128)} %copy.93) | copy-start | bytes 7864324
  402.2 6.4 copy-start.23
  402.2 9.3 %copy-start.20 = (f32[256,256]{1,0:T(8,128)S(1)}, f32[256,256]{1,0:T(8,128)}, u32[]{:S(2)}) copy-start(f32[256,256]{1,0:T(8,128)} %copy-done.18) | copy-start | bytes 786436
  427.5 6.1 copy-start.3
  433.6 6.2 copy-start.17
  433.6 6.2 copy-start.26
  433.7 6.4 copy-start.30
  433.7 7.8 %copy-start.14 = (bf16[1,256,2560]{2,1,0:T(8,128)(2,1)S(1)}, bf16[1,256,2560]{2,1,0:T(8,128)(2,1)}, u32[]{:S(2)}) copy-start(bf16[1,256,2560]{2,1,0:T(8,128)(2,1)} %param.16) | copy-start | bytes 3932164
  441.4 310.1 %all-reduce.20.cloned.1.call-start = ((), (), s32[]{:S(2)}) async-start(), calls=%async_computation.3 | async-start | bytes 6553600 | tf_op jit(solution)/shard_map/psum | solution.py:160
  487.2 5.9 collective-permute-start.1
  751.5 5.8 copy-start.1
  751.5 4.0 copy-start.21
  751.5 4.6 copy-start.25
  751.5 5.2 copy-start.28
Sparse Core Ops, SparseCore 0:
  9.6 28.2 all-gather.7
  40.6 150.7 all-gather.9
  231.9 148.6 all-gather.11
  383.1 101.2 reduce-scatter.1
  490.8 123.6 all-reduce.21
  617.9 133.5 all-reduce.19
where the time goes:
time: 772 us; the launch traced here: 764 us
  waiting for transfers between devices  505 us (65%)
  matrix products  92.2 us (12%)
  other arithmetic  69.3 us (9%)
  local copies, waits for them, and re-layouts  47.8 us (6%)
  blocking collectives  22.7 us (3%)
  between operations  15.6 us (2%)
  starting transfers between devices  11.3 us (1%)
    all_gather x2, waiting for transfers between devices, entering_2(): everything = jax.tree.map(lambda part: lax.all_gather(part, axis), value)  199 us
    psum x1, waiting for transfers between devices, body(): weight_grad = lax.psum(weight_piece, 'seq')  137 us
    psum x1, waiting for transfers between devices, body(): lax.psum((filter_part, grad_norm, head_part), ('seq', 'dp'))  120 us
    dot_general x3, matrix products, finish(): inside = jnp.einsum('hcts,cshp->cthp', weights, scaled, precision=HIGHEST)  43.8 us
    reduce_scatter x1, waiting for transfers between devices, body(): lax.psum_scatter(lax.dot_general(normed_low, cotangent, (((0,), (0,)), ((...  38.5 us
    select_n x16, other arithmetic, lap(): return jax.tree.map(lambda a, b: jnp.where(reached, a, b), new, before)  27.8 us
    unnamed x1, blocking collectives  22.7 us
    dot_general x3, matrix products, prepare(): jnp.einsum('hcs,cshp,csn->chpn', to_end, scaled, key_side, precision=HIGH...  16.7 us
  transfers between devices with their start and end apart: 9, of which 8 were waited for; matrix products, arithmetic and copies ran while one was open for 21% of the time, Pallas kernels for 0%

commit v1 on v0

--- a/solution.py
+++ b/solution.py
@@ -157,7 +157,11 @@
         scatter_dimension=0,
         tiled=True,
     )
-    weight_grad = lax.psum(weight_piece, "seq")
+    weight_grad = weight_piece
+    for hop in (1, 2, 4):
+        weight_grad = weight_grad + lax.ppermute(
+            weight_grad, "seq", [(dev, dev ^ hop) for dev in range(8)]
+        )
     second = pull_second(normed_grad)
     (
         grad_activated,

time: 772 us -> 893 us (1.16)
  waiting for transfers between devices: 505 us -> 611 us
  other arithmetic: 69.3 us -> 79.3 us
    ppermute x0 -> x3, waiting for transfers between devices: none -> 190 us  [body(): lax.ppermute(weight_grad, 'seq', [(dev, dev ^ hop) for dev in range(8)])]
    psum x1 -> x0, waiting for transfers between devices: 137 us -> none  [body(): weight_grad = lax.psum(weight_piece, 'seq')]
    all_gather x2, waiting for transfers between devices: 199 us -> 282 us  [entering_2(): everything = jax.tree.map(lambda part: lax.all_gather(part, axis), value)]
    psum x1, waiting for transfers between devices: 120 us -> 92.6 us  [body(): lax.psum((filter_part, grad_norm, head_part), ('seq', 'dp'))]
    add x0 -> x3, other arithmetic: none -> 14.4 us  [body(): weight_grad + lax.ppermute(weight_grad, 'seq', [(dev, dev ^ hop) for dev...]
  transfers between devices with their start and end apart: 9 -> 11, of which waited for: 8 -> 8; matrix products, arithmetic and copies ran while one was open for 21% -> 18% of each run, Pallas kernels for 0% -> 0%
where the time goes in v1:
time: 893 us; the launch traced here: 885 us
  waiting for transfers between devices  611 us (68%)
  matrix products  90.8 us (10%)
  other arithmetic  79.3 us (9%)
  local copies, waits for them, and re-layouts  50.7 us (6%)
  blocking collectives  22.7 us (3%)
  between operations  15.4 us (2%)
  starting transfers between devices  14.1 us (2%)
    all_gather x2, waiting for transfers between devices, entering_2(): everything = jax.tree.map(lambda part: lax.all_gather(part, axis), value)  282 us
    ppermute x3, waiting for transfers between devices, body(): lax.ppermute(weight_grad, 'seq', [(dev, dev ^ hop) for dev in range(8)])  190 us
    psum x1, waiting for transfers between devices, body(): lax.psum((filter_part, grad_norm, head_part), ('seq', 'dp'))  92.6 us
    dot_general x3, matrix products, finish(): inside = jnp.einsum('hcts,cshp->cthp', weights, scaled, precision=HIGHEST)  43.4 us
    reduce_scatter x1, waiting for transfers between devices, body(): lax.psum_scatter(lax.dot_general(normed_low, cotangent, (((0,), (0,)), ((...  39.4 us
    select_n x16, other arithmetic, lap(): return jax.tree.map(lambda a, b: jnp.where(reached, a, b), new, before)  25.8 us
    unnamed x1, blocking collectives  22.7 us
  transfers between devices with their start and end apart: 11, of which 8 were waited for; matrix products, arithmetic and copies ran while one was open for 18% of the time, Pallas kernels for 0%

profile of v1, /device:TPU:0, one launch (start us, length us, event | category | flops | bytes accessed | tf_op | source)
XLA Modules:
  0.0 885.2 jit_solution(12450058970826772173)
XLA Ops:
  8.8 4.9 collective-permute-start
  20.2 3.0 fusion.21
  24.7 1.9 slice.95
  26.6 3.2 copy.94
  29.8 5.0 fusion.69
  34.9 3.0 all-gather.8.cloned.1.call-done
  37.9 5.5 fusion.48
  43.4 4.7 all-to-all-start
  49.7 22.7 %all-reduce.15 = f32[320]{0:T(512)S(1)} all-reduce(f32[320]{0:T(512)S(1)} %dynamic-update-slice), channel_id=3, replica_groups=mesh['seq'=8,'dp'=4] {'seq'}, use_global_device_ids=true, to_apply=%add.15 | all-reduce | flops 320 | bytes 2560
  72.5 1.9 copy.100
  75.9 3.5 all-to-all-done
  79.4 3.2 copy.93
  82.7 108.5 %all-gather.10.cloned.1.call-done = f32[320,64,128]{2,1,0:T(8,128)} async-done(((f32[40,64,128]{2,1,0:T(8,128)}), f32[320,64,128]{2,1,0:T(8,128)}) %all-gather.10.cloned.1.call-update) | async-done | bytes 10485776 | tf_op jit(solution)/shard_map/all_gather | solution.py:24
  191.2 13.2 %while.30 = (s32[]{:T(128)}, f32[40,64,128]{2,1,0:T(8,128)S(1)}, s32[]{:T(128)}, f32[8,40]{1,0:T(8,128)S(1)}, f32[8,40,64,128]{3,2,1,0:T(8,128)}, /*index=5*/s32[]{:T(128)}, s32[]{:T(128)}) while((s32[]{:T(128)}, f32[40,64,128]{2,1,0:T(8,128)S(1)}, s32[]{:T(128)}, f32[8,40]{1,0:T(8,128)S(1)}, f32[8,40,64,128]{3,2,1,0:T(8,128)}, ...), condition=%wide.region_3.4_spmd.clone, body=%wide.region_2.3_spmd.clone.sunk | while | flops 1310724 | bytes 3932745 | solution.py:37
  192.8 1.6 fusion.137
  194.5 1.6 fusion.137
  204.4 3.3 fusion.93
  207.8 15.5 %multiply_reduce_fusion.8 = (f32[256]{0:T(256)S(1)}, f32[256]{0:T(256)S(1)}, f32[1,256,40,64]{1,3,2,0:T(8,128)S(1)}, f32[1,256,40,64]{1,3,2,0:T(8,128)}) fusion(f32[1,256,40,64]{1,3,2,0:T(8,128)} %bitcast.259, f32[40,64]{1,0:T(8,128)S(1)} %mul.591, f32[1,256,40,64]{1,3,2,0:T(8,128)} %bitcast.262, f32[1,256,40,64]{1,3,2,0:T(8,128)S(1)} %bitcast.254, ...), kind=kOutput, calls=%fused_computation.79 | convolution fusion | flops 2030960128 | bytes 18813088 | tf_op jit(solution)/shard_map/jvp(hcts,cshp->cthp)/dot_general | solution.py:87
  223.3 3.0 broadcast_multiply_fusion.5
  226.4 6.5 fusion.86
  233.0 5.0 fusion.44
  238.1 3.7 convert_element_type.75
  241.7 4.8 copy.129
  246.6 2.1 copy-done.12
  248.6 15.3 %fusion.8 = (f32[40,256]{1,0:T(8,128)S(1)}, f32[40,256]{1,0:T(8,128)}, f32[256,256]{1,0:T(8,128)S(1)}) fusion(f32[40,256]{1,0:T(8,128)S(1)} %get-tuple-element.347, f32[256,256]{1,0:T(8,128)S(1)} %fusion.98, pred[256,256]{1,0:T(8,128)(4,1)S(1)} %iota_compare_fusion, f32[256,40,64]{0,2,1:T(8,128)S(1)} %bitcast.256, f32[256,40]{0,1:T(8,128)S(1)} %fusion.106, ...), kind=kOutput, calls=%fused_computation.13 | convolution fusion | flops 2037428224 | bytes 5996544 | tf_op jit(solution)/shard_map/transpose(jvp(hcts,cshp->cthp))/dot_general | solution.py:87
  263.9 3.3 copy.101
  267.2 3.2 copy.117
  270.4 4.5 fusion.33
  275.5 3.2 copy.106
  278.7 1.6 fusion.101
  280.3 6.0 fusion.83
  287.7 3.4 fusion.29
  292.5 2.7 fusion.26
  295.2 39.4 %reduce-scatter.2.cloned.1.call-done = f32[640,1280]{1,0:T(8,128)} async-done(((f32[2560,1280]{1,0:T(8,128)}), f32[640,1280]{1,0:T(8,128)}) %reduce-scatter.2.cloned.1.call-update) | async-done | bytes 3276816 | tf_op jit(solution)/shard_map/reduce_scatter | solution.py:152
  336.0 173.8 %all-gather.12.cloned.1.call-done = f32[320,64,128]{2,1,0:T(8,128)} async-done(((f32[40,64,128]{2,1,0:T(8,128)}), f32[320,64,128]{2,1,0:T(8,128)}) %all-gather.12.cloned.1.call-update) | async-done | bytes 10485776 | tf_op jit(solution)/shard_map/all_gather | solution.py:24
  509.8 19.1 %while.31 = (s32[]{:T(128)}, f32[40,64,128]{2,1,0:T(8,128)S(1)}, s32[]{:T(128)}, f32[8,40]{1,0:T(8,128)}, f32[8,40,64,128]{3,2,1,0:T(8,128)}, /*index=5*/s32[]{:T(128)}, s32[]{:T(128)}, s32[]{:T(128)}, s32[]{:T(128)}) while((s32[]{:T(128)}, f32[40,64,128]{2,1,0:T(8,128)S(1)}, s32[]{:T(128)}, f32[8,40]{1,0:T(8,128)}, ...), condition=%wide.region_8.9_spmd.clone, body=%wide.region_7.8_spmd.clone.sunk | while | flops 1310728 | bytes 3932807 | solution.py:37
  529.4 5.6 fusion.39
  536.0 2.5 reduce-window.16
  538.7 12.6 %multiply_reduce_fusion.5 = (f32[40]{0:T(128)S(1)}, f32[256,40]{0,1:T(8,128)S(1)}, f32[1,256,40,64]{1,3,2,0:T(8,128)}) fusion(f32[1,256,40,64]{1,3,2,0:T(8,128)} %get-tuple-element.342, f32[1,256,40,64]{1,3,2,0:T(8,128)} %bitcast.252, f32[256,40]{0,1:T(8,128)S(1)} %fusion.106, f32[256,40]{0,1:T(8,128)S(1)} %get-tuple-element.346, ...), kind=kOutput, calls=%fused_computation.75 | convolution fusion | flops 2025707520 | bytes 10977440 | tf_op jit(solution)/shard_map/transpose(jvp(hcts,cshp->cthp))/dot_general | solution.py:87
  551.4 4.3 add.287
  555.8 3.4 copy.103
  559.6 6.2 fusion.80
  565.8 4.9 multiply_reduce_fusion.4
  571.7 56.6 %collective-permute-done.3 = f32[640,1280]{1,0:T(8,128)} collective-permute-done((f32[640,1280]{1,0:T(8,128)}, f32[640,1280]{1,0:T(8,128)}, u32[]{:S(2)}, u32[]{:S(2)}) %collective-permute-start.3) | collective-permute-done | bytes 3276832 | tf_op jit(solution)/shard_map/ppermute | solution.py:162
  628.2 5.0 add.288
  643.6 133.2 %collective-permute-done.4 = f32[640,1280]{1,0:T(8,128)} collective-permute-done((f32[640,1280]{1,0:T(8,128)}, f32[640,1280]{1,0:T(8,128)}, u32[]{:S(2)}, u32[]{:S(2)}) %collective-permute-start.4) | collective-permute-done | bytes 3276832 | tf_op jit(solution)/shard_map/ppermute | solution.py:162
  776.8 5.0 add.289
  781.8 92.6 %all-reduce.19.cloned.1.call-done = (f32[5,2816]{1,0:T(8,128)}, f32[2560]{0:T(1024)}, f32[3,40]{1,0:T(4,128)}) async-done(((f32[5,2816]{1,0:T(8,128)}, f32[2560]{0:T(1024)}, f32[3,40]{1,0:T(4,128)}), (f32[5,2816]{1,0:T(8,128)}, f32[2560]{0:T(1024)}, f32[3,40]{1,0:T(4,128)})) %all-reduce.19.cloned.1.call-update) | async-done | bytes 67056 | tf_op jit(solution)/shard_map/psum | solution.py:197
  (207 shorter events, 62.7 us)
Async XLA Ops:
  7.2 30.7 %copy-start = (bf16[640,1280]{1,0:T(8,128)(2,1)S(1)}, bf16[640,1280]{1,0:T(8,128)(2,1)}, u32[]{:S(2)}) copy-start(bf16[640,1280]{1,0:T(8,128)(2,1)} %param.24) | copy-start | bytes 4915204
  7.2 12.7 %copy-start.23 = (bf16[1,256,2816]{2,1,0:T(8,128)(2,1)S(1)}, bf16[1,256,2816]{2,1,0:T(8,128)(2,1)}, u32[]{:S(2)}) copy-start(bf16[1,256,2816]{2,1,0:T(8,128)(2,1)} %param.15) | copy-start | bytes 4325380
  7.2 30.7 %all-gather.8.cloned.1.call-start = ((), (), s32[]{:S(2)}) async-start(), calls=%async_computation.3 | async-start | bytes 3276800 | tf_op jit(solution)/shard_map/all_gather | solution.py:143
  7.9 183.3 %all-gather.10.cloned.1.call-start = ((), (), s32[]{:S(2)}) async-start(), calls=%async_computation.4 | async-start | bytes 11796480 | tf_op jit(solution)/shard_map/all_gather | solution.py:24
  8.8 11.1 %collective-permute-start = (bf16[3,2816]{1,0:T(4,128)(2,1)S(1)}, bf16[3,2816]{1,0:T(4,128)(2,1)S(1)}, u32[]{:S(2)}, u32[]{:S(2)}) collective-permute-start(bf16[3,2816]{1,0:T(4,128)(2,1)S(1)} %slice_bitcast_fusion), channel_id=1, source_target_pairs={{0,4},{4,8},{8,12},{12,16},{16,20},{20,24},{24,28},{1,5},{5,9},{9,... | collective-permute-start | bytes 50696 | tf_op jit(solution)/shard_map/ppermute | solution.py:19
  16.5 3.7 copy-start.36
  17.8 5.4 copy-start.38
  18.8 227.7 %copy-start.31 = (f32[40,256]{1,0:T(8,128)}, f32[40,256]{1,0:T(8,128)S(1)}, u32[]{:S(2)}) copy-start(f32[40,256]{1,0:T(8,128)S(1)} %get-tuple-element.347) | copy-start | bytes 122884
  43.4 4.8 copy-start.45
  43.4 29.1 %copy-start.15 = (bf16[1,256,2560]{2,1,0:T(8,128)(2,1)S(1)}, bf16[1,256,2560]{2,1,0:T(8,128)(2,1)}, u32[]{:S(2)}) copy-start(bf16[1,256,2560]{2,1,0:T(8,128)(2,1)} %param.16) | copy-start | bytes 3932164
  43.4 36.1 %all-to-all-start = ((f32[4,256,640]{2,1,0:T(8,128)}), f32[4,256,640]{2,1,0:T(8,128)}, u32[]{:S(2)}, u32[]{:S(2)}) async-start(f32[4,256,640]{2,1,0:T(8,128)} %bitcast.271), calls=%async_computation | async-start | bytes 5242880 | tf_op jit(solution)/shard_map/all_to_all | solution.py:149
  48.1 26.3 %copy-start.29 = (f32[2560]{0:T(1024)S(1)}, f32[2560]{0:T(1024)}, u32[]{:S(2)}) copy-start(f32[2560]{0:T(1024)} %param.23) | copy-start | bytes 30724
  48.1 286.5 %reduce-scatter.2.cloned.1.call-start = ((), (), s32[]{:S(2)}) async-start(), calls=%async_computation.2 | async-start | bytes 16384000 | tf_op jit(solution)/shard_map/reduce_scatter | solution.py:152
  74.5 172.0 %copy-start.27 = (pred[256,256]{1,0:T(8,128)(4,1)}, pred[256,256]{1,0:T(8,128)(4,1)S(1)}, u32[]{:S(2)}) copy-start(pred[256,256]{1,0:T(8,128)(4,1)S(1)} %iota_compare_fusion) | copy-start | bytes 196612
  75.9 170.6 %copy-start.25 = (f32[256,256]{1,0:T(8,128)}, f32[256,256]{1,0:T(8,128)S(1)}, u32[]{:S(2)}) copy-start(f32[256,256]{1,0:T(8,128)S(1)} %fusion.98) | copy-start | bytes 786436
  204.4 18.8 %copy-start.42 = (f32[8,40]{1,0:T(8,128)}, f32[8,40]{1,0:T(8,128)S(1)}, u32[]{:S(2)}) copy-start(f32[8,40]{1,0:T(8,128)S(1)} %get-tuple-element.513) | copy-start | bytes 3844
  207.7 15.5 %copy-start.19 = (f32[256,40,64]{0,2,1:T(8,128)}, f32[256,40,64]{0,2,1:T(8,128)S(1)}, u32[]{:S(2)}) copy-start(f32[256,40,64]{0,2,1:T(8,128)S(1)} %fusion.93) | copy-start | bytes 7864324
  207.7 15.5 %copy-start.10 = (f32[1,256,4,640]{1,3,2,0:T(8,128)S(1)}, f32[1,256,4,640]{1,3,2,0:T(8,128)}, u32[]{:S(2)}) copy-start(f32[1,256,4,640]{1,3,2,0:T(8,128)} %copy.93) | copy-start | bytes 7864324
  207.8 15.5 %copy-start.13 = (f32[1,256,2560]{1,2,0:T(8,128)S(1)}, f32[1,256,2560]{1,2,0:T(8,128)}, u32[]{:S(2)}) copy-start(f32[1,256,2560]{1,2,0:T(8,128)} %copy.100) | copy-start | bytes 7864324
  232.9 276.9 %all-gather.12.cloned.1.call-start = ((), (), s32[]{:S(2)}) async-start(), calls=%async_computation.5 | async-start | bytes 11796480 | tf_op jit(solution)/shard_map/all_gather | solution.py:24
  238.0 636.4 %all-reduce.19.cloned.1.call-start = ((), (), s32[]{:S(2)}) async-start(), calls=%async_computation.6 | async-start | bytes 208896 | tf_op jit(solution)/shard_map/psum | solution.py:197
  241.7 4.8 copy-start.8
  241.7 6.9 copy-start.12
  278.7 8.9 %copy-start.9 = (f32[1,256,40,64]{1,3,2,0:T(8,128)S(1)}, f32[1,256,40,64]{1,3,2,0:T(8,128)}, u32[]{:S(2)}) copy-start(f32[1,256,40,64]{1,3,2,0:T(8,128)} %get-tuple-element.358) | copy-start | bytes 7864324
  278.7 8.9 %copy-start.11 = (f32[1,256,4,640]{1,3,2,0:T(8,128)S(1)}, f32[1,256,4,640]{1,3,2,0:T(8,128)}, u32[]{:S(2)}) copy-start(f32[1,256,4,640]{1,3,2,0:T(8,128)} %copy.93) | copy-start | bytes 7864324
  278.7 8.9 %copy-start.35 = (f32[256]{0:T(256)S(1)}, f32[256]{0:T(256)}, u32[]{:S(2)}) copy-start(f32[256]{0:T(256)} %copy-done.34) | copy-start | bytes 3076
  287.6 3.9 copy-start.17
  287.6 4.9 copy-start.18
  287.6 4.9 copy-start.30
  334.6 216.8 %collective-permute-start.2 = (f32[640,1280]{1,0:T(8,128)}, f32[640,1280]{1,0:T(8,128)}, u32[]{:S(2)}, u32[]{:S(2)}) collective-permute-start(f32[640,1280]{1,0:T(8,128)} %reduce-scatter.2.cloned.1.call-done), channel_id=1, source_target_pairs={{0,4},{4,0},{8,12},{12,8},{16,20},{20,16},{24,28},{28,24},{1,5},{5... | collective-permute-start | bytes 9830408 | tf_op jit(solution)/shard_map/ppermute | solution.py:162
  529.4 5.6 copy-start.39
  529.4 6.5 copy-start.33
  529.4 9.3 %copy-start.26 = (f32[256,256]{1,0:T(8,128)S(1)}, f32[256,256]{1,0:T(8,128)}, u32[]{:S(2)}) copy-start(f32[256,256]{1,0:T(8,128)} %copy-done.25) | copy-start | bytes 786436
  529.4 9.3 %copy-start.28 = (pred[256,256]{1,0:T(8,128)(4,1)S(1)}, pred[256,256]{1,0:T(8,128)(4,1)}, u32[]{:S(2)}) copy-start(pred[256,256]{1,0:T(8,128)(4,1)} %copy-done.27) | copy-start | bytes 196612
  529.4 9.3 %copy-start.32 = (f32[40,256]{1,0:T(8,128)S(1)}, f32[40,256]{1,0:T(8,128)}, u32[]{:S(2)}) copy-start(f32[40,256]{1,0:T(8,128)} %copy-done.31) | copy-start | bytes 122884
  538.7 12.6 %copy-start.21 = (f32[640,1280]{1,0:T(8,128)S(1)}, f32[640,1280]{1,0:T(8,128)}, u32[]{:S(2)}) copy-start(f32[640,1280]{1,0:T(8,128)} %reduce-scatter.2.cloned.1.call-done) | copy-start | bytes 9830404
  555.7 72.6 %collective-permute-start.3 = (f32[640,1280]{1,0:T(8,128)}, f32[640,1280]{1,0:T(8,128)}, u32[]{:S(2)}, u32[]{:S(2)}) collective-permute-start(f32[640,1280]{1,0:T(8,128)} %add.287), channel_id=1, source_target_pairs={{0,8},{4,12},{8,0},{12,4},{16,24},{20,28},{24,16},{28,20},{1,9},{5... | collective-permute-start | bytes 9830408 | tf_op jit(solution)/shard_map/ppermute | solution.py:162
  555.8 3.6 copy-start.24
  555.8 3.6 copy-start.37
  555.8 3.6 copy-start.41
  559.2 6.6 copy-start.3
  571.6 65.7 %copy-start.4 = (f32[256,2816]{1,0:T(8,128)}, f32[256,2816]{1,0:T(8,128)S(1)}, u32[]{:S(2)}) copy-start(f32[256,2816]{1,0:T(8,128)S(1)} %get-tuple-element.351) | copy-start | bytes 8650756
  571.6 65.7 %copy-start.5 = (f32[256,2816]{1,0:T(8,128)}, f32[256,2816]{1,0:T(8,128)S(1)}, u32[]{:S(2)}) copy-start(f32[256,2816]{1,0:T(8,128)S(1)} %get-tuple-element.352) | copy-start | bytes 8650756
  571.6 65.7 %copy-start.6 = (f32[256,2816]{1,0:T(8,128)}, f32[256,2816]{1,0:T(8,128)S(1)}, u32[]{:S(2)}) copy-start(f32[256,2816]{1,0:T(8,128)S(1)} %get-tuple-element.353) | copy-start | bytes 8650756
  571.6 63.1 %copy-start.44 = (f32[40]{0:T(128)S(1)}, f32[40]{0:T(128)}, u32[]{:S(2)}) copy-start(f32[40]{0:T(128)} %param.21) | copy-start | bytes 484
  633.3 143.5 %collective-permute-start.4 = (f32[640,1280]{1,0:T(8,128)}, f32[640,1280]{1,0:T(8,128)}, u32[]{:S(2)}, u32[]{:S(2)}) collective-permute-start(f32[640,1280]{1,0:T(8,128)} %add.288), channel_id=1, source_target_pairs={{0,16},{4,20},{8,24},{12,28},{16,0},{20,4},{24,8},{28,12},{1,17},{... | collective-permute-start | bytes 9830408 | tf_op jit(solution)/shard_map/ppermute | solution.py:162
  634.9 6.0 collective-permute-start.1
  642.4 236.1 %copy-start.1 = (bf16[640,1280]{1,0:T(8,128)(2,1)S(1)}, bf16[640,1280]{1,0:T(8,128)(2,1)}, u32[]{:S(2)}) copy-start(bf16[640,1280]{1,0:T(8,128)(2,1)} %param.24) | copy-start | bytes 4915204
  (9 other events, 23.9 us)
Sparse Core Ops, SparseCore 0:
  9.6 28.2 all-gather.7
  40.6 150.5 all-gather.9
  233.0 101.4 reduce-scatter.1
  337.2 172.5 all-gather.11
  641.0 233.2 all-reduce.18
